TPU v7x, 32 devices: a whole 2x2x4 slice. The times are simulated.
32 devices in a mesh: member: 2 (over x), region: 16 (over z, y, core).
Axes of the slice: x: 2, y: 2, z: 4, core: 2. Of those that a mesh axis runs over, the one named last changes fastest.
Arguments:
- mesh_nodes: bfloat16 [16384, 512], P(('member', 'region')), parts along dimension 0, may hold values from -6 to 6
- mesh_edges: bfloat16 [32768, 512], P('region'), may hold values from -6 to 6
- grid_nodes: bfloat16 [12288, 512], P(('member', 'region')), parts along dimension 0, may hold values from -6 to 6
- grid_edges: bfloat16 [18432, 512], P('region'), may hold values from -6 to 6
- boundary: int32 [16, 32], P('region'), may hold values from 0 to 511
- mesh_need: int32 [16, 16, 8], P('region'), may hold values from 0 to 31
- mesh_sender: int32 [16, 2048], P('region'), may hold values from 0 to 639, as said below
- mesh_receiver: int32 [16, 2048], P('region'), may hold values from 0 to 511
- mesh_live: int32 [16], P('region'), may hold values from 512 to 2048, as said below
- grid_need: int32 [16, 4, 8], P('region'), may hold values from 0 to 31
- grid_sender: int32 [16, 1152], P('region'), may hold values from 0 to 543, as said below
- grid_receiver: int32 [16, 1152], P('region'), may hold values from 0 to 383
- process_edge_in: bfloat16 [1536, 512], replicated, may hold values from -0.15625 to 0.15625
- process_edge_bias: float32 [512], replicated, may hold values from -3 to 3
- process_edge_out: bfloat16 [512, 512], replicated, may hold values from -0.25 to 0.25
- process_edge_gain: float32 [512], replicated, may hold values from 0.5 to 1.5
- process_node_in: bfloat16 [1024, 512], replicated, may hold values from -0.1875 to 0.1875
- process_node_bias: float32 [512], replicated, may hold values from -3 to 3
- process_node_out: bfloat16 [512, 512], replicated, may hold values from -0.25 to 0.25
- process_node_gain: float32 [512], replicated, may hold values from 0.5 to 1.5
- decode_edge_in: bfloat16 [1536, 512], replicated, may hold values from -0.15625 to 0.15625
- decode_edge_bias: float32 [512], replicated, may hold values from -3 to 3
- decode_edge_out: bfloat16 [512, 512], replicated, may hold values from -0.25 to 0.25
- decode_edge_gain: float32 [512], replicated, may hold values from 0.5 to 1.5
- decode_node_in: bfloat16 [1024, 512], replicated, may hold values from -0.1875 to 0.1875
- decode_node_bias: float32 [512], replicated, may hold values from -3 to 3
- decode_node_out: bfloat16 [512, 512], replicated, may hold values from -0.25 to 0.25
- decode_node_gain: float32 [512], replicated, may hold values from 0.5 to 1.5
Outputs:
- mesh_out: bfloat16 [16384, 512], P(('member', 'region')), parts along dimension 0
- grid_out: bfloat16 [12288, 512], P(('member', 'region')), parts along dimension 0
There are 2 independent parts, one for each index of `member`. A program takes and returns all parts, laid end to end along the dimension named above; an argument that names none is the same for every part. Nothing has to cross between parts.
Inputs may be any that keep to these rules, and one draw needn't show every extreme that they name: The first mesh_live[d] slots of region d are live and the rest are padding; in every draw some region has all 2048 slots live. `mesh_sender`: a value below 512 names a node of the region itself; 512 + s * 8 + k names the k-th node that the region reads from region s; most slots name the region's own nodes, most remote reads come from its four neighbours, and a few reach any region. `grid_sender`: a value below 512 names a node of the region's mesh_out; 512 + j * 8 + k names the k-th node read from its j-th neighbour; most edges name the region's own nodes.
All inputs are finite; a program needn't handle non-finite values.
Results may differ from a plain program's by a relative error of at most 0.007.
Values may be sent and summed in bfloat16 or wider, within the bound.
A program may use at most 64 MiB of HBM per device.

v0:
```python
import functools

import jax
import jax.numpy as jnp
from jax import lax
from jax.experimental import pallas as pl
from jax.experimental.pallas import tpu as pltpu
from jax.sharding import PartitionSpec as P

F32 = jnp.float32
BF16 = jnp.bfloat16
OFFSETS = (-2, -1, 1, 2)
LANES = 128
BLOCK = 1024
GRID_BLOCK = 384


def dot(a, b):
    return jnp.dot(a, b, preferred_element_type=F32)


def silu(x):
    half = 0.5 * x
    return half * jnp.tanh(half) + half


def normed(hidden, w_out, gain):
    projected = dot(hidden, w_out)
    centred = projected - jnp.mean(projected, axis=-1, keepdims=True)
    spread = jnp.mean(centred * centred, axis=-1, keepdims=True)
    return centred * lax.rsqrt(spread + 0.25) * gain


def lane_hot(column, first, count):
    lane = lax.broadcasted_iota(jnp.int32, column.shape, 1) + first
    pieces = [
        jnp.where(column == lane + start, 1.0, 0.0).astype(BF16) for start in range(0, count, LANES)
    ]
    return pieces[0] if len(pieces) == 1 else jnp.concatenate(pieces, axis=1)


def row_hot(row, count):
    place = lax.broadcasted_iota(jnp.int32, (count, row.shape[1]), 0)
    return jnp.where(place == row, 1.0, 0.0).astype(BF16)


def up(count, unit=LANES):
    return -(-count // unit) * unit


def kernel(
    sizes,
    live_ref,
    boundary_hbm,
    need_hbm,
    gneed_hbm,
    mesh_nodes_hbm,
    mesh_edges_hbm,
    grid_nodes_hbm,
    grid_edges_hbm,
    mesh_sender_hbm,
    mesh_receiver_hbm,
    grid_sender_hbm,
    grid_receiver_hbm,
    pe_in, pe_b, pe_out, pe_g,
    pn_in, pn_b, pn_out, pn_g,
    de_in, de_b, de_out, de_g,
    dn_in, dn_b, dn_out, dn_g,
    mesh_out_ref,
    grid_out_ref,
    idx, offer_row, need_raw, gneed_raw, own, edges, gnodes, gedges, send_row, recv_row, gsend_row, grecv_row,
    w_s, w_r, table, w_po, w_pn, w_pno,
    w_ds, w_dr, gtable, w_do, w_dn, w_dno,
    vec,
    col_s, col_r, col_gs, col_gr,
    pre, gpre, npre, gnpre, total, gtotal,
    pub, everyone, rem, pub_out, arrived, grem,
    mesh_out_own, write_sem, load_sem, send_sem, recv_sem, pass_send_sem, pass_recv_sem, out_send_sem, out_recv_sem,
):
    regions, offer, pair, n, m, edge_count, g, gedge_count, rows_at = sizes
    me = lax.axis_index("region")

    barrier = pltpu.get_barrier_semaphore()

    def greet(step, carry):
        pl.semaphore_signal(
            barrier,
            inc=1,
            device_id={"region": lax.rem(me + step, regions)},
            device_id_type=pl.DeviceIdType.MESH,
        )
        return carry

    lax.fori_loop(1, regions, greet, 0)

    loads = {}

    def load(name, source, target):
        copy = pltpu.make_async_copy(source, target, load_sem.at[len(loads)])
        copy.start()
        loads[name] = copy

    load("own", mesh_nodes_hbm, own)
    load("offer", boundary_hbm, offer_row)
    load("srow", mesh_sender_hbm, send_row)
    load("row", mesh_receiver_hbm, recv_row)
    load("gsrow", grid_sender_hbm, gsend_row)
    load("grow", grid_receiver_hbm, grecv_row)
    load("need", need_hbm, need_raw)
    load("gneed", gneed_hbm, gneed_raw)
    load("w_s", pe_in.at[pl.ds(0, m)], w_s)
    load("w_r", pe_in.at[pl.ds(m, m)], w_r)
    load("w_e", pe_in.at[pl.ds(2 * m, m)], table.at[pl.ds(2 * n, m)])
    load("edges", mesh_edges_hbm, edges)
    for at, one in enumerate((pe_b, pe_g, pn_b, pn_g, de_b, de_g, dn_b, dn_g)):
        load(("vec", at), one, vec.at[at])
    load("gnodes", grid_nodes_hbm, gnodes)
    load("w_dr", de_in.at[pl.ds(m, m)], w_dr)
    load("w_de", de_in.at[pl.ds(2 * m, m)], gtable.at[pl.ds(g, m)])
    load("gedges", grid_edges_hbm, gedges)
    load("w_pn", pn_in, w_pn)
    load("w_dn", dn_in, w_dn)
    load("w_po", pe_out, w_po)
    load("w_pno", pn_out, w_pno)
    load("w_ds", de_in.at[pl.ds(0, m)], w_ds)
    load("w_do", de_out, w_do)
    load("w_dno", dn_out, w_dno)

    idx[...] = jnp.zeros_like(idx)
    for name, source, start in (
        ("offer", offer_row, rows_at["boundary"]),
        ("need", need_raw, rows_at["need"]),
        ("gneed", gneed_raw, rows_at["gneed"]),
    ):
        loads[name].wait()
        idx[start : start + source.shape[0], : source.shape[1]] = source[...]
    for name, source, start in (
        ("srow", send_row, rows_at["sender"]),
        ("row", recv_row, rows_at["receiver"]),
        ("gsrow", gsend_row, rows_at["gsender"]),
        ("grow", grecv_row, rows_at["greceiver"]),
    ):
        loads[name].wait()
        for k in range(source.shape[1] // LANES):
            idx[start + k : start + k + 1, :] = source[:, k * LANES : (k + 1) * LANES]
    across = jnp.transpose(idx[...])

    def across_part(start):
        return pltpu.roll(across, LANES - start, 1)

    def column(row):
        return jnp.broadcast_to(across[:, row : row + 1], (LANES, LANES))

    offer_col = column(rows_at["boundary"])[:offer]

    loads["own"].wait()
    pub[...] = dot(lane_hot(offer_col, 0, n), own[...]).astype(BF16)
    pl.semaphore_wait(barrier, regions - 1)

    half = regions // 2
    partner = me + 1 - 2 * lax.rem(me, 2)

    def block_of(region):
        return everyone.at[pl.ds(pl.multiple_of(region * offer, offer), offer)]

    def send(step, carry):
        pltpu.make_async_remote_copy(
            src_ref=pub,
            dst_ref=block_of(me),
            send_sem=send_sem,
            recv_sem=recv_sem,
            device_id={"region": lax.rem(me + 2 * step, regions)},
            device_id_type=pl.DeviceIdType.MESH,
        ).start()
        return carry

    def to_partner(source, region):
        pltpu.make_async_remote_copy(
            src_ref=source,
            dst_ref=block_of(region),
            send_sem=pass_send_sem,
            recv_sem=pass_recv_sem,
            device_id={"region": partner},
            device_id_type=pl.DeviceIdType.MESH,
        ).start()

    lax.fori_loop(1, half, send, 0)
    to_partner(pub, me)
    everyone[pl.ds(pl.multiple_of(me * offer, offer), offer), :] = pub[...]

    def chosen(table, rows, columns, by_row):
        count = rows * columns
        row = lax.broadcasted_iota(jnp.int32, (rows, columns, LANES), 0).reshape(count, LANES)
        lane = lax.broadcasted_iota(jnp.int32, (count, LANES), 1)
        inner = lax.broadcasted_iota(jnp.int32, (rows, columns, LANES), 1).reshape(count, LANES)
        down, along = (row, inner) if by_row else (inner, row)
        lines = dot(jnp.where(lane == down, 1.0, 0.0).astype(BF16), table.astype(F32).astype(BF16))
        picked = jnp.sum(jnp.where(lane == along, lines, 0.0), axis=1, keepdims=True)
        return jnp.broadcast_to(picked.astype(jnp.int32), (count, LANES)) + row * offer

    need_at, gneed_at = rows_at["need"], rows_at["gneed"]
    slots, gslots = regions * pair, len(OFFSETS) * pair
    need_col = chosen(across_part(need_at), regions, pair, True)
    gneed_col = chosen(across_part(gneed_at), len(OFFSETS), pair, False)
    for start, target, count in (
        (rows_at["sender"], col_s, edge_count),
        (rows_at["receiver"], col_r, edge_count),
        (rows_at["gsender"], col_gs, gedge_count),
        (rows_at["greceiver"], col_gr, gedge_count),
    ):
        for k in range(count // LANES):
            target[pl.ds(k * LANES, LANES), :] = column(start + k)

    loads["w_s"].wait()
    table[pl.ds(0, n), :] = dot(own[...], w_s[...]).astype(BF16)
    loads["w_r"].wait()
    table[pl.ds(n, n), :] = dot(own[...], w_r[...]).astype(BF16)
    loads["w_e"].wait()
    loads["edges"].wait()
    for at in range(8):
        loads[("vec", at)].wait()

    def first(block, carry):
        rows = pl.ds(pl.multiple_of(block * BLOCK, BLOCK), BLOCK)
        inputs = jnp.concatenate(
            [lane_hot(col_s[rows, :], 0, n), lane_hot(col_r[rows, :], 0, n), edges[rows, :]], axis=1
        )
        pre[rows, :] = dot(inputs, table[...]) + vec[0]
        return carry

    lax.fori_loop(0, edge_count // BLOCK, first, 0)

    loads["gnodes"].wait()
    loads["w_dr"].wait()
    gtable[pl.ds(0, g), :] = dot(gnodes[...], w_dr[...]).astype(BF16)
    loads["w_de"].wait()
    loads["gedges"].wait()

    def gfirst(block, carry):
        rows = pl.ds(pl.multiple_of(block * GRID_BLOCK, GRID_BLOCK), GRID_BLOCK)
        inputs = jnp.concatenate([lane_hot(col_gr[rows, :], 0, g), gedges[rows, :]], axis=1)
        gpre[rows, :] = dot(inputs, gtable[...]) + vec[4]
        return carry

    lax.fori_loop(0, gedge_count // GRID_BLOCK, gfirst, 0)
    loads["w_pn"].wait()
    npre[...] = dot(own[...], w_pn[pl.ds(0, m), :]) + vec[2]
    loads["w_dn"].wait()
    gnpre[...] = dot(gnodes[...], w_dn[pl.ds(0, m), :]) + vec[6]
    for name in ("w_po", "w_pno", "w_ds", "w_do", "w_dno"):
        loads[name].wait()
    total[...] = jnp.zeros_like(total)
    rem[...] = jnp.zeros_like(rem)
    grem[...] = jnp.zeros_like(grem)
    gtotal[...] = jnp.zeros_like(gtotal)

    direct = everyone.at[pl.ds(0, (half - 1) * offer)]
    pltpu.make_async_copy(direct, direct, recv_sem).wait()

    def forward(step, carry):
        region = lax.rem(me + 2 * step, regions)
        to_partner(block_of(region), region)
        return carry

    lax.fori_loop(1, half, forward, 0)
    passed = everyone.at[pl.ds(0, half * offer)]
    pltpu.make_async_copy(passed, passed, pass_recv_sem).wait()
    pltpu.make_async_copy(passed, passed, pass_send_sem).wait()
    pltpu.make_async_copy(direct, direct, send_sem).wait()
    wanted = dot(lane_hot(need_col, 0, up(regions * offer)), everyone[...])
    rem[pl.ds(0, slots), :] = dot(wanted.astype(BF16), w_s[...]).astype(BF16)
    live = live_ref[0]

    def second(block, carry):
        rows = pl.ds(pl.multiple_of(block * BLOCK, BLOCK), BLOCK)
        act = pre[rows, :] + dot(lane_hot(col_s[rows, :], n, rem.shape[0]), rem[...])
        message = normed(silu(act).astype(BF16), w_po[...], vec[1]) + edges[rows, :].astype(F32)
        place = lax.broadcasted_iota(jnp.int32, (1, BLOCK), 1) + block * BLOCK
        receivers = jnp.where(place < live, recv_row[:, rows], -1)
        total[...] += dot(row_hot(receivers, n), message.astype(BF16))
        return carry

    lax.fori_loop(0, edge_count // BLOCK, second, 0)

    act = npre[...] + dot(total[...].astype(BF16), w_pn[pl.ds(m, m), :])
    updated = own[...].astype(F32) + normed(silu(act).astype(BF16), w_pno[...], vec[3])
    mesh_out_own[...] = updated
    writing = pltpu.make_async_copy(mesh_out_own, mesh_out_ref, write_sem)
    writing.start()
    table[pl.ds(n, n), :] = updated.astype(BF16)

    pub_out[...] = dot(lane_hot(offer_col, 0, n), table[pl.ds(n, n), :]).astype(BF16)
    copies = []
    for slot, offset in enumerate(OFFSETS):
        copy = pltpu.make_async_remote_copy(
            src_ref=pub_out,
            dst_ref=arrived.at[pl.ds(slot * offer, offer)],
            send_sem=out_send_sem.at[slot],
            recv_sem=out_recv_sem.at[slot],
            device_id={"region": lax.rem(me - offset + regions, regions)},
            device_id_type=pl.DeviceIdType.MESH,
        )
        copy.start()
        copies.append(copy)
    table[pl.ds(0, n), :] = dot(table[pl.ds(n, n), :], w_ds[...]).astype(BF16)

    def glocal(block, carry):
        rows = pl.ds(pl.multiple_of(block * GRID_BLOCK, GRID_BLOCK), GRID_BLOCK)
        gpre[rows, :] += dot(lane_hot(col_gs[rows, :], 0, n), table[pl.ds(0, n), :])
        return carry

    lax.fori_loop(0, gedge_count // GRID_BLOCK, glocal, 0)
    for copy in copies:
        copy.wait()
    wanted = dot(lane_hot(gneed_col, 0, arrived.shape[0]), arrived[...])
    grem[pl.ds(0, gslots), :] = dot(wanted.astype(BF16), w_ds[...]).astype(BF16)

    def gsecond(block, carry):
        rows = pl.ds(pl.multiple_of(block * GRID_BLOCK, GRID_BLOCK), GRID_BLOCK)
        act = gpre[rows, :] + dot(lane_hot(col_gs[rows, :], n, grem.shape[0]), grem[...])
        message = normed(silu(act).astype(BF16), w_do[...], vec[5]) + gedges[rows, :].astype(F32)
        gtotal[...] += dot(row_hot(grecv_row[:, rows], g), message.astype(BF16))
        return carry

    lax.fori_loop(0, gedge_count // GRID_BLOCK, gsecond, 0)
    act = gnpre[...] + dot(gtotal[...].astype(BF16), w_dn[pl.ds(m, m), :])
    grid_out_ref[...] = (
        gnodes[...].astype(F32) + normed(silu(act).astype(BF16), w_dno[...], vec[7])
    )
    writing.wait()


def local(
    mesh_nodes, mesh_edges, grid_nodes, grid_edges,
    boundary, mesh_need, mesh_sender, mesh_receiver, mesh_live,
    grid_need, grid_sender, grid_receiver,
    *weights,
):
    regions = mesh_need.shape[1]
    pair = mesh_need.shape[2]
    offer = boundary.shape[1]
    n, m = mesh_nodes.shape
    g = grid_nodes.shape[0]
    edge_count = mesh_edges.shape[0]
    gedge_count = grid_edges.shape[0]
    slots = regions * pair
    rows_at = {}
    at = 0
    for name, count in (
        ("sender", edge_count // LANES),
        ("receiver", edge_count // LANES),
        ("gsender", gedge_count // LANES),
        ("greceiver", gedge_count // LANES),
        ("need", pair),
        ("gneed", len(OFFSETS)),
        ("boundary", 1),
    ):
        rows_at[name] = at
        at += count
    assert at <= LANES and regions <= LANES
    weights = [w if w.ndim == 2 else w.reshape(1, -1) for w in weights]

    sizes = (regions, offer, pair, n, m, edge_count, g, gedge_count, rows_at)
    v = pltpu.VMEM
    arrived_rows = up(len(OFFSETS) * offer)
    scratch = [
        v((LANES, LANES), jnp.int32), v((1, offer), jnp.int32), v((pair, regions), jnp.int32), v((len(OFFSETS), pair), jnp.int32),
        v((n, m), BF16), v((edge_count, m), BF16), v((g, m), BF16), v((gedge_count, m), BF16),
        v((1, edge_count), jnp.int32), v((1, edge_count), jnp.int32), v((1, gedge_count), jnp.int32), v((1, gedge_count), jnp.int32),
        v((m, m), BF16), v((m, m), BF16), v((2 * n + m, m), BF16), v((m, m), BF16), v((2 * m, m), BF16), v((m, m), BF16),
        v((m, m), BF16), v((m, m), BF16), v((g + m, m), BF16), v((m, m), BF16), v((2 * m, m), BF16), v((m, m), BF16),
        v((8, 1, m), F32),
        v((edge_count, LANES), jnp.int32), v((edge_count, LANES), jnp.int32),
        v((gedge_count, LANES), jnp.int32), v((gedge_count, LANES), jnp.int32),
        v((edge_count, m), F32), v((gedge_count, m), F32), v((n, m), F32), v((g, m), F32), v((n, m), F32), v((g, m), F32),
        v((offer, m), BF16), v((up(regions * offer), m), BF16), v((up(slots), m), BF16),
        v((offer, m), BF16), v((arrived_rows, m), BF16), v((LANES, m), BF16),
        v((n, m), F32), pltpu.SemaphoreType.DMA, pltpu.SemaphoreType.DMA((40,)),
        pltpu.SemaphoreType.DMA, pltpu.SemaphoreType.DMA, pltpu.SemaphoreType.DMA, pltpu.SemaphoreType.DMA,
        pltpu.SemaphoreType.DMA((len(OFFSETS),)), pltpu.SemaphoreType.DMA((len(OFFSETS),)),
    ]
    hbm = pl.BlockSpec(memory_space=pl.ANY)
    mesh_out, grid_out = pl.pallas_call(
        functools.partial(kernel, sizes),
        out_shape=(
            jax.ShapeDtypeStruct((n, m), F32),
            jax.ShapeDtypeStruct((g, m), F32),
        ),
        in_specs=[pl.BlockSpec(memory_space=pltpu.SMEM)] + [hbm] * 27,
        out_specs=(hbm, pl.BlockSpec(memory_space=pltpu.VMEM)),
        scratch_shapes=scratch,
        compiler_params=pltpu.CompilerParams(
            collective_id=0, has_side_effects=True, vmem_limit_bytes=56 * 1024 * 1024
        ),
        name="layer",
    )(
        mesh_live, boundary, jnp.swapaxes(mesh_need[0], 0, 1), grid_need[0],
        mesh_nodes, mesh_edges, grid_nodes, grid_edges,
        mesh_sender, mesh_receiver, grid_sender, grid_receiver,
        *weights,
    )
    return mesh_out.astype(BF16), grid_out.astype(BF16)


def solution(mesh):
    both = P(("member", "region"), None)
    by = P("region", None)
    return jax.shard_map(
        local,
        mesh=mesh,
        in_specs=(
            both, by, both, by, by, P("region", None, None), by, by, P("region"),
            P("region", None, None), by, by,
        ) + (P(),) * 16,
        out_specs=(both, both),
        check_vma=False,
    )
```

profile of v0, /device:TPU:0, one launch (start us, length us, event | category | flops | bytes accessed | tf_op | source)
XLA Modules:
  0.0 35.9 jit_solution(13171949129944004938)
XLA Ops:
  1.3 31.7 %layer.1 = (f32[512,512]{1,0:T(8,128)}, f32[384,512]{1,0:T(8,128)}) custom-call(s32[1]{0:T(128)S(6)} %copy.30.live_ref, s32[1,32]{1,0:T(1,128)} %boundary_hbm.1, s32[8,16]{1,0:T(8,128)} %bitcast.12, s32[4,8]{1,0:T(4,128)} %bitcast.13, bf16[512,512]{1,0:T(8,128)(2,1)} %mesh_nodes_hbm.1, bf16[2048,512]{1,0:T(8,128)(2,1)} %mesh_edges_hbm.1, ...), custom_call_target="tpu_custom_call" | custom-call | tf_op jit(solution)/shard_map/layer/pallas_call | solution.py:383
  33.0 0.0 copy-start
  33.0 2.2 %convert_element_type.6 = bf16[512,512]{1,0:T(8,128)(2,1)} convert(f32[512,512]{1,0:T(8,128)} %get-tuple-element.4) | non-fusion elementwise | flops 262144 | bytes 1572864 | tf_op jit(solution)/shard_map/convert_element_type | solution.py:402
  35.1 0.0 copy-done
  35.1 0.8 %convert_element_type.7 = bf16[384,512]{1,0:T(8,128)(2,1)} convert(f32[384,512]{1,0:T(8,128)S(1)} %copy-done) | non-fusion elementwise | flops 196608 | bytes 1179648 | tf_op jit(solution)/shard_map/convert_element_type | solution.py:402
Async XLA Ops:
  33.0 2.2 %copy-start = (f32[384,512]{1,0:T(8,128)S(1)}, f32[384,512]{1,0:T(8,128)}, u32[]{:S(2)}) copy-start(f32[384,512]{1,0:T(8,128)} %get-tuple-element.5) | copy-start | bytes 2359300
where the time goes:
time: 36.1 us; the launch traced here: 35.9 us
  Pallas kernels  31.7 us (88%)
  other arithmetic  2.95 us (8%)
  between operations  1.3 us (4%)
    pallas_call x1, Pallas kernels, local(): pl.pallas_call(functools.partial(kernel, sizes), out_shape=(jax.ShapeDtyp...  31.7 us
    convert_element_type x2, other arithmetic, local(): return (mesh_out.astype(BF16), grid_out.astype(BF16))  2.95 us

commit v1 on v0

v1 whole, which is shorter than its diff:
```python
import functools

import jax
import jax.numpy as jnp
from jax import lax
from jax.experimental import pallas as pl
from jax.experimental.pallas import tpu as pltpu
from jax.sharding import PartitionSpec as P

F32 = jnp.float32
BF16 = jnp.bfloat16
I32 = jnp.int32
OFFSETS = (-2, -1, 1, 2)
LANES = 128
SUB = 8
BLOCK = 512
GRID_BLOCK = 384


def dot(a, b):
    return jnp.dot(a, b, preferred_element_type=F32)


def silu(x):
    half = 0.5 * x
    return half * jnp.tanh(half) + half


def normed(hidden, w_out, gain):
    projected = dot(hidden, w_out)
    centred = projected - jnp.mean(projected, axis=-1, keepdims=True)
    spread = jnp.mean(centred * centred, axis=-1, keepdims=True)
    return centred * lax.rsqrt(spread + 0.25) * gain


def lane_hot(column, first, count):
    lane = lax.broadcasted_iota(I32, column.shape, 1) + first
    pieces = [
        jnp.where(column == lane + start, 1.0, 0.0).astype(BF16) for start in range(0, count, LANES)
    ]
    return pieces[0] if len(pieces) == 1 else jnp.concatenate(pieces, axis=1)


def row_hot(row, count):
    place = lax.broadcasted_iota(I32, (count, row.shape[1]), 0)
    return jnp.where(place == row, 1.0, 0.0).astype(BF16)


def column_of(scalars):
    sub = lax.broadcasted_iota(I32, (SUB, LANES), 0)
    pieces = []
    for start in range(0, len(scalars), SUB):
        piece = jnp.full((SUB, LANES), scalars[start], I32)
        for k in range(1, SUB):
            piece = jnp.where(sub == k, scalars[start + k], piece)
        pieces.append(piece)
    return pieces[0] if len(pieces) == 1 else jnp.concatenate(pieces, axis=0)


def up(count, unit=LANES):
    return -(-count // unit) * unit


def kernel(
    sizes,
    live_hbm,
    boundary_hbm,
    need_hbm,
    gneed_hbm,
    mesh_nodes_hbm,
    mesh_edges_hbm,
    grid_nodes_hbm,
    grid_edges_hbm,
    mesh_sender_hbm,
    mesh_receiver_hbm,
    grid_sender_hbm,
    grid_receiver_hbm,
    pe_in, pe_b, pe_out, pe_g,
    pn_in, pn_b, pn_out, pn_g,
    de_in, de_b, de_out, de_g,
    dn_in, dn_b, dn_out, dn_g,
    mesh_out_ref,
    grid_out_ref,
    live, offers, need, gneed, senders, receivers, gsenders, greceivers,
    own, edges, gnodes, gedges, recv_row, grecv_row,
    w_pe, w_po, w_pn, w_pno, w_de, w_do, w_dn, w_dno, vec,
    tab_s, tab_r, gtab_s, gtab_r, picked, gpicked,
    pre, gpre, npre, gnpre, total, gtotal, updated,
    pub, everyone, pub_out, arrived, mesh_stage, grid_stage,
    write_sem, load_sem, send_sem, recv_sem, pass_send_sem, pass_recv_sem, out_send_sem, out_recv_sem,
):
    regions, offer, pair, n, m, edge_count, g, gedge_count = sizes
    slots, gslots = regions * pair, len(OFFSETS) * pair
    chunks = m // LANES
    me = lax.axis_index("region")

    loads = {}

    def load(name, source, target):
        copy = pltpu.make_async_copy(source, target, load_sem.at[len(loads)])
        copy.start()
        loads[name] = copy

    load("offers", boundary_hbm, offers)
    load("own", mesh_nodes_hbm, own)

    barrier = pltpu.get_barrier_semaphore()

    def greet(step, carry):
        pl.semaphore_signal(
            barrier,
            inc=1,
            device_id={"region": lax.rem(me + step, regions)},
            device_id_type=pl.DeviceIdType.MESH,
        )
        return carry

    lax.fori_loop(1, regions, greet, 0)

    load("w_s", pe_in.at[pl.ds(0, m)], w_pe.at[pl.ds(0, m)])
    load("w_r", pe_in.at[pl.ds(m, m)], w_pe.at[pl.ds(m, m)])
    for at, one in enumerate((pe_b, pe_g, pn_b, pn_g, de_b, de_g, dn_b, dn_g)):
        load(("vec", at), one, vec.at[at])
    load("receivers", mesh_receiver_hbm, receivers)
    load("senders", mesh_sender_hbm, senders)
    load("greceivers", grid_receiver_hbm, greceivers)
    load("gsenders", grid_sender_hbm, gsenders)
    load("need", need_hbm, need)
    load("gneed", gneed_hbm, gneed)
    load("live", live_hbm, live)
    load("w_e", pe_in.at[pl.ds(2 * m, m)], w_pe.at[pl.ds(2 * m, m)])
    for start in range(0, edge_count, BLOCK):
        load(("edges", start), mesh_edges_hbm.at[pl.ds(start, BLOCK)], edges.at[pl.ds(start, BLOCK)])
    load("w_pn", pn_in, w_pn)
    load("gnodes", grid_nodes_hbm, gnodes)
    load("w_de", de_in, w_de)
    load("gedges", grid_edges_hbm, gedges)
    load("w_dn", dn_in, w_dn)
    load("recv_row", mesh_receiver_hbm, recv_row)
    load("grecv_row", grid_receiver_hbm, grecv_row)
    load("w_po", pe_out, w_po)
    load("w_pno", pn_out, w_pno)
    load("w_do", de_out, w_do)
    load("w_dno", dn_out, w_dno)

    loads["offers"].wait()
    offer_col = column_of([offers[0, k] for k in range(offer)])
    offer_hot = lane_hot(offer_col, 0, n)
    loads["own"].wait()
    pub[...] = dot(offer_hot, own[...]).astype(BF16)
    pl.semaphore_wait(barrier, regions - 1)

    half = regions // 2
    partner = me + 1 - 2 * lax.rem(me, 2)

    def block_of(region):
        return everyone.at[pl.ds(pl.multiple_of(region * offer, offer), offer)]

    def send(step, carry):
        pltpu.make_async_remote_copy(
            src_ref=pub,
            dst_ref=block_of(me),
            send_sem=send_sem,
            recv_sem=recv_sem,
            device_id={"region": lax.rem(me + 2 * step, regions)},
            device_id_type=pl.DeviceIdType.MESH,
        ).start()
        return carry

    def to_partner(source, region):
        pltpu.make_async_remote_copy(
            src_ref=source,
            dst_ref=block_of(region),
            send_sem=pass_send_sem,
            recv_sem=pass_recv_sem,
            device_id={"region": partner},
            device_id_type=pl.DeviceIdType.MESH,
        ).start()

    lax.fori_loop(1, half, send, 0)
    to_partner(pub, me)
    everyone[pl.ds(pl.multiple_of(me * offer, offer), offer), :] = pub[...]

    def scatter_rows(target, first, rows, values):
        for c in range(chunks):
            target[pl.ds(first * chunks + c, rows, stride=chunks), :] = values[:, c * LANES : (c + 1) * LANES]

    def gathered_rows(source, first, rows):
        return jnp.concatenate(
            [source[pl.ds(first * chunks + c, rows, stride=chunks), :] for c in range(chunks)], axis=1
        )

    def pick(target, table, index, first, count):
        def one(at, carry):
            row = index[0, first + at]
            target[pl.ds(at * chunks, chunks), :] = table[pl.ds(row * chunks, chunks), :]
            return carry

        lax.fori_loop(0, count, one, 0, unroll=True)

    for at in range(8):
        loads[("vec", at)].wait()
    loads["w_r"].wait()
    scatter_rows(tab_r, 0, n, dot(own[...], w_pe[pl.ds(m, m), :]) + vec[0])
    loads["w_s"].wait()
    scatter_rows(tab_s, 0, n, dot(own[...], w_pe[pl.ds(0, m), :]))
    for name in ("receivers", "senders", "greceivers", "gsenders", "need", "gneed", "live"):
        loads[name].wait()
    need_col = column_of([need[k, s] + s * offer for s in range(regions) for k in range(pair)])
    gneed_col = column_of([gneed[j, k] + j * offer for j in range(len(OFFSETS)) for k in range(pair)])
    loads["w_e"].wait()
    for start in range(0, edge_count, BLOCK):
        loads[("edges", start)].wait()
    for start in range(0, edge_count, BLOCK):
        rows = pl.ds(start, BLOCK)
        pick(picked.at[start // BLOCK % 2], tab_r, receivers, start, BLOCK)
        pre[rows, :] = dot(edges[rows, :], w_pe[pl.ds(2 * m, m), :]) + gathered_rows(
            picked.at[start // BLOCK % 2], 0, BLOCK
        )

    for name in ("w_pn", "gnodes", "w_de", "gedges", "w_dn"):
        loads[name].wait()
    npre[...] = dot(own[...], w_pn[pl.ds(0, m), :]) + vec[2]
    scatter_rows(gtab_r, 0, g, dot(gnodes[...], w_de[pl.ds(m, m), :]) + vec[4])
    for start in range(0, gedge_count, GRID_BLOCK):
        rows = pl.ds(start, GRID_BLOCK)
        slot = gpicked.at[start // GRID_BLOCK % 2]
        pick(slot, gtab_r, greceivers, start, GRID_BLOCK)
        gpre[rows, :] = dot(gedges[rows, :], w_de[pl.ds(2 * m, m), :]) + gathered_rows(slot, 0, GRID_BLOCK)
    gnpre[...] = dot(gnodes[...], w_dn[pl.ds(0, m), :]) + vec[6]

    for name in ("recv_row", "grecv_row", "w_po", "w_pno", "w_do", "w_dno"):
        loads[name].wait()

    direct = everyone.at[pl.ds(0, (half - 1) * offer)]
    pltpu.make_async_copy(direct, direct, recv_sem).wait()

    def forward(step, carry):
        region = lax.rem(me + 2 * step, regions)
        to_partner(block_of(region), region)
        return carry

    lax.fori_loop(1, half, forward, 0)
    passed = everyone.at[pl.ds(0, half * offer)]
    pltpu.make_async_copy(passed, passed, pass_recv_sem).wait()
    pltpu.make_async_copy(passed, passed, pass_send_sem).wait()
    pltpu.make_async_copy(direct, direct, send_sem).wait()
    wanted = dot(lane_hot(need_col, 0, regions * offer), everyone[...])
    scatter_rows(tab_s, n, slots, dot(wanted.astype(BF16), w_pe[pl.ds(0, m), :]))

    for start in range(0, edge_count, BLOCK):
        rows = pl.ds(start, BLOCK)
        slot = picked.at[start // BLOCK % 2]
        pick(slot, tab_s, senders, start, BLOCK)
        act = pre[rows, :] + gathered_rows(slot, 0, BLOCK)
        message = normed(silu(act).astype(BF16), w_po[...], vec[1]) + edges[rows, :].astype(F32)
        place = lax.broadcasted_iota(I32, (1, BLOCK), 1) + start
        targets = jnp.where(place < live[0], recv_row[:, start : start + BLOCK], -1)
        part = dot(row_hot(targets, n), message.astype(BF16))
        total[...] = part if start == 0 else total[...] + part

    act = npre[...] + dot(total[...].astype(BF16), w_pn[pl.ds(m, m), :])
    updated[...] = (
        own[...].astype(F32) + normed(silu(act).astype(BF16), w_pno[...], vec[3])
    ).astype(BF16)
    pub_out[...] = dot(offer_hot, updated[...]).astype(BF16)
    copies = []
    for slot, offset in enumerate(OFFSETS):
        copy = pltpu.make_async_remote_copy(
            src_ref=pub_out,
            dst_ref=arrived.at[pl.ds(slot * offer, offer)],
            send_sem=out_send_sem.at[slot],
            recv_sem=out_recv_sem.at[slot],
            device_id={"region": lax.rem(me - offset + regions, regions)},
            device_id_type=pl.DeviceIdType.MESH,
        )
        copy.start()
        copies.append(copy)
    writing = pltpu.make_async_copy(updated, mesh_out_ref, write_sem.at[0])
    writing.start()
    scatter_rows(gtab_s, 0, n, dot(updated[...], w_de[pl.ds(0, m), :]))
    for copy in copies:
        copy.wait()
    wanted = dot(lane_hot(gneed_col, 0, arrived.shape[0]), arrived[...])
    scatter_rows(gtab_s, n, gslots, dot(wanted.astype(BF16), w_de[pl.ds(0, m), :]))

    for start in range(0, gedge_count, GRID_BLOCK):
        rows = pl.ds(start, GRID_BLOCK)
        slot = gpicked.at[start // GRID_BLOCK % 2]
        pick(slot, gtab_s, gsenders, start, GRID_BLOCK)
        act = gpre[rows, :] + gathered_rows(slot, 0, GRID_BLOCK)
        message = normed(silu(act).astype(BF16), w_do[...], vec[5]) + gedges[rows, :].astype(F32)
        part = dot(row_hot(grecv_row[:, start : start + GRID_BLOCK], g), message.astype(BF16))
        gtotal[...] = part if start == 0 else gtotal[...] + part

    act = gnpre[...] + dot(gtotal[...].astype(BF16), w_dn[pl.ds(m, m), :])
    grid_stage[...] = (
        gnodes[...].astype(F32) + normed(silu(act).astype(BF16), w_dno[...], vec[7])
    ).astype(BF16)
    gwriting = pltpu.make_async_copy(grid_stage, grid_out_ref, write_sem.at[1])
    gwriting.start()
    writing.wait()
    gwriting.wait()


def local(
    mesh_nodes, mesh_edges, grid_nodes, grid_edges,
    boundary, mesh_need, mesh_sender, mesh_receiver, mesh_live,
    grid_need, grid_sender, grid_receiver,
    *weights,
):
    regions = mesh_need.shape[1]
    pair = mesh_need.shape[2]
    offer = boundary.shape[1]
    n, m = mesh_nodes.shape
    g = grid_nodes.shape[0]
    edge_count = mesh_edges.shape[0]
    gedge_count = grid_edges.shape[0]
    slots = regions * pair
    gslots = len(OFFSETS) * pair
    chunks = m // LANES
    weights = [w if w.ndim == 2 else w.reshape(1, -1) for w in weights]

    sizes = (regions, offer, pair, n, m, edge_count, g, gedge_count)
    v = pltpu.VMEM
    s = pltpu.SMEM
    dma = pltpu.SemaphoreType.DMA
    scratch = [
        s((1,), I32), s((1, offer), I32), s((pair, regions), I32), s((len(OFFSETS), pair), I32),
        s((1, edge_count), I32), s((1, edge_count), I32), s((1, gedge_count), I32), s((1, gedge_count), I32),
        v((n, m), BF16), v((edge_count, m), BF16), v((g, m), BF16), v((gedge_count, m), BF16),
        v((1, edge_count), I32), v((1, gedge_count), I32),
        v((3 * m, m), BF16), v((m, m), BF16), v((2 * m, m), BF16), v((m, m), BF16),
        v((3 * m, m), BF16), v((m, m), BF16), v((2 * m, m), BF16), v((m, m), BF16),
        v((8, 1, m), F32),
        v(((n + slots) * chunks, LANES), F32), v((n * chunks, LANES), F32),
        v(((n + gslots) * chunks, LANES), F32), v((g * chunks, LANES), F32),
        v((2, BLOCK * chunks, LANES), F32), v((2, GRID_BLOCK * chunks, LANES), F32),
        v((edge_count, m), F32), v((gedge_count, m), F32), v((n, m), F32), v((g, m), F32),
        v((n, m), F32), v((g, m), F32), v((n, m), BF16),
        v((offer, m), BF16), v((regions * offer, m), BF16), v((offer, m), BF16),
        v((len(OFFSETS) * offer, m), BF16), v((8, LANES), BF16), v((g, m), BF16),
        dma((2,)), dma((44,)),
        dma, dma, dma, dma,
        dma((len(OFFSETS),)), dma((len(OFFSETS),)),
    ]
    hbm = pl.BlockSpec(memory_space=pltpu.HBM)
    return pl.pallas_call(
        functools.partial(kernel, sizes),
        out_shape=(
            jax.ShapeDtypeStruct((n, m), BF16),
            jax.ShapeDtypeStruct((g, m), BF16),
        ),
        in_specs=[hbm] * 28,
        out_specs=(pl.BlockSpec(memory_space=pl.ANY),) * 2,
        scratch_shapes=scratch,
        compiler_params=pltpu.CompilerParams(
            collective_id=0, has_side_effects=True, vmem_limit_bytes=56 * 1024 * 1024
        ),
        name="layer",
    )(
        mesh_live, boundary, jnp.swapaxes(mesh_need[0], 0, 1), grid_need[0],
        mesh_nodes, mesh_edges, grid_nodes, grid_edges,
        mesh_sender, mesh_receiver, grid_sender, grid_receiver,
        *weights,
    )


def solution(mesh):
    both = P(("member", "region"), None)
    by = P("region", None)
    return jax.shard_map(
        local,
        mesh=mesh,
        in_specs=(
            both, by, both, by, by, P("region", None, None), by, by, P("region"),
            P("region", None, None), by, by,
        ) + (P(),) * 16,
        out_specs=(both, both),
        check_vma=False,
    )
```

time: 36.1 us -> 35.8 us (level)
  local copies, waits for them, and re-layouts: 0.01 us -> 3.63 us
  other arithmetic: 2.95 us -> 0 us
  Pallas kernels: 31.7 us -> 30.7 us
    unnamed x2, local copies, waits for them, and re-layouts: 0.01 us -> 3.63 us
    convert_element_type x2 -> x0, other arithmetic: 2.95 us -> none  [local(): return (mesh_out.astype(BF16), grid_out.astype(BF16))]
    pallas_call x1, Pallas kernels: 31.7 us -> 30.7 us  [local(): pl.pallas_call(functools.partial(kernel, sizes), out_shape=(jax.ShapeDtyp...]
where the time goes in v1:
time: 35.8 us; the launch traced here: 35.6 us
  Pallas kernels  30.7 us (86%)
  local copies, waits for them, and re-layouts  3.63 us (10%)
  between operations  1.3 us (4%)
    pallas_call x1, Pallas kernels, local(): pl.pallas_call(functools.partial(kernel, sizes), out_shape=(jax.ShapeDtyp...  30.7 us
    unnamed x2, local copies, waits for them, and re-layouts  3.63 us

profile of v1, /device:TPU:0, one launch (start us, length us, event | category | flops | bytes accessed | tf_op | source)
XLA Modules:
  0.0 35.6 jit_solution(3531165241353869047)
XLA Ops:
  1.3 30.7 %layer.1 = (bf16[512,512]{1,0:T(8,128)(2,1)}, bf16[384,512]{1,0:T(8,128)(2,1)}) custom-call(s32[1]{0:T(128)S(6)} %copy.32.live_hbm, s32[1,32]{1,0:T(1,128)} %boundary_hbm.1, s32[8,16]{1,0:T(8,128)} %bitcast.12, s32[4,8]{1,0:T(4,128)} %bitcast.13, bf16[512,512]{1,0:T(8,128)(2,1)} %mesh_nodes_hbm.1, bf16[2048,512]{1,0:T(8,128)(2,1)} %mesh_edges_hbm.1, ...), custom_call_target="tpu_custom_call" | custom-call | tf_op jit(solution)/shard_map/layer/pallas_call | solution.py:348
  32.0 1.9 %copy.33 = bf16[512,512]{1,0:T(8,128)(2,1)} copy(bf16[512,512]{1,0:T(8,128)(2,1)} %get-tuple-element.4) | data formatting | bytes 1048576
  33.9 1.8 %copy.34 = bf16[384,512]{1,0:T(8,128)(2,1)} copy(bf16[384,512]{1,0:T(8,128)(2,1)} %get-tuple-element.5) | data formatting | bytes 786432

commit v2 on v1

v2 whole, which is shorter than its diff:
```python
import functools

import jax
import jax.numpy as jnp
from jax import lax
from jax.experimental import pallas as pl
from jax.experimental.pallas import tpu as pltpu
from jax.sharding import PartitionSpec as P

F32 = jnp.float32
BF16 = jnp.bfloat16
I32 = jnp.int32
OFFSETS = (-2, -1, 1, 2)
LANES = 128
SUB = 8
BLOCK = 512
GRID_BLOCK = 384


def dot(a, b):
    return jnp.dot(a, b, preferred_element_type=F32)


def silu_of_half(half):
    half = half.astype(BF16)
    return half * jnp.tanh(half) + half


def normed(hidden, w_centred, gain):
    centred = dot(hidden, w_centred)
    spread = jnp.mean(centred * centred, axis=-1, keepdims=True)
    return centred * lax.rsqrt(spread + 0.25) * gain


def centre(w_ref):
    w = w_ref[...].astype(F32)
    w_ref[...] = (w - jnp.mean(w, axis=-1, keepdims=True)).astype(BF16)


def lane_hot(column, first, count):
    lane = lax.broadcasted_iota(I32, column.shape, 1) + first
    pieces = [
        jnp.where(column == lane + start, 1.0, 0.0).astype(BF16) for start in range(0, count, LANES)
    ]
    return pieces[0] if len(pieces) == 1 else jnp.concatenate(pieces, axis=1)


def row_mask(row, count):
    place = lax.broadcasted_iota(I32, (count, row.shape[1]), 0)
    return jnp.where(place == row, 1.0, 0.0)


def row_hot(row, count):
    return row_mask(row, count).astype(BF16)


def column_of(scalars):
    sub = lax.broadcasted_iota(I32, (SUB, LANES), 0)
    pieces = []
    for start in range(0, len(scalars), SUB):
        piece = jnp.full((SUB, LANES), scalars[start], I32)
        for k in range(1, SUB):
            piece = jnp.where(sub == k, scalars[start + k], piece)
        pieces.append(piece)
    return pieces[0] if len(pieces) == 1 else jnp.concatenate(pieces, axis=0)


def up(count, unit=LANES):
    return -(-count // unit) * unit


def kernel(
    sizes,
    live_hbm,
    boundary_hbm,
    need_hbm,
    gneed_hbm,
    mesh_nodes_hbm,
    mesh_edges_hbm,
    grid_nodes_hbm,
    grid_edges_hbm,
    mesh_sender_hbm,
    mesh_receiver_hbm,
    grid_sender_hbm,
    grid_receiver_hbm,
    pe_in, pe_b, pe_out, pe_g,
    pn_in, pn_b, pn_out, pn_g,
    de_in, de_b, de_out, de_g,
    dn_in, dn_b, dn_out, dn_g,
    updated, gtotal, gnpre, gnodes, w_dn, w_dno, vec,
    live, offers, need, gneed, senders, receivers, gsenders, greceivers,
    own, edges, gedges, recv_row, send_row, grecv_row, gsend_row, scaled_rows,
    w_pe, w_po, w_pn, w_pno, w_de, w_do,
    tab_s, tab_r, gtab_s, gtab_r, picked, gpicked,
    pre, gpre, npre, npre_offer, total, hot, ghot, rem,
    pub, everyone, pub_out, arrived,
    load_sem, index_sem, send_sem, pass_sem, recv_sem, out_send_sem, out_recv_sem,
):
    regions, offer, pair, n, m, edge_count, g, gedge_count = sizes
    slots, gslots = regions * pair, len(OFFSETS) * pair
    chunks = m // LANES
    me = lax.axis_index("region")

    loads = {}

    def load(name, source, target):
        copy = pltpu.make_async_copy(source, target, load_sem.at[len(loads)])
        copy.start()
        loads[name] = copy

    load("offers", boundary_hbm, offers)
    load("own", mesh_nodes_hbm, own)

    barrier = pltpu.get_barrier_semaphore()

    def greet(step, carry):
        pl.semaphore_signal(
            barrier,
            inc=1,
            device_id={"region": lax.rem(me + step, regions)},
            device_id_type=pl.DeviceIdType.MESH,
        )
        return carry

    lax.fori_loop(1, regions, greet, 0)

    load("w_s", pe_in.at[pl.ds(0, m)], w_pe.at[pl.ds(0, m)])
    load("w_r", pe_in.at[pl.ds(m, m)], w_pe.at[pl.ds(m, m)])
    for at, one in enumerate((pe_b, pe_g, pn_b, pn_g, de_b, de_g, dn_b, dn_g)):
        load(("vec", at), one, vec.at[at])
    load("recv_row", mesh_receiver_hbm, recv_row)
    load("send_row", mesh_sender_hbm, send_row)
    load("grecv_row", grid_receiver_hbm, grecv_row)
    load("gsend_row", grid_sender_hbm, gsend_row)
    load("need", need_hbm, need)
    load("gneed", gneed_hbm, gneed)
    load("live", live_hbm, live)
    load("w_e", pe_in.at[pl.ds(2 * m, m)], w_pe.at[pl.ds(2 * m, m)])
    for start in range(0, edge_count, BLOCK):
        load(("edges", start), mesh_edges_hbm.at[pl.ds(start, BLOCK)], edges.at[pl.ds(start, BLOCK)])
    load("w_pn", pn_in, w_pn)
    load("gnodes", grid_nodes_hbm, gnodes)
    load("w_de", de_in, w_de)
    load("w_po", pe_out, w_po)
    load("w_pno", pn_out, w_pno)
    load("w_dn", dn_in, w_dn)
    load("gedges", grid_edges_hbm, gedges)
    load("w_do", de_out, w_do)
    load("w_dno", dn_out, w_dno)

    loads["offers"].wait()
    offer_col = column_of([offers[0, k] for k in range(offer)])
    offer_hot = lane_hot(offer_col, 0, n)
    loads["own"].wait()
    pub[...] = dot(offer_hot, own[...]).astype(BF16)
    pl.semaphore_wait(barrier, regions - 1)

    chips, chip, core = regions // 2, me // 2, lax.rem(me, 2)

    rings = chips // 2
    ring, lane_y = chip // 2, lax.rem(chip, 2)
    hops = sorted(
        ((dz, dy) for dz in range(rings) for dy in range(2) if dz or dy),
        key=lambda hop: (-min(hop[0], rings - hop[0]) - hop[1], -hop[0], -hop[1]),
    )

    def chip_to(step):
        dz, dy = hops[step]
        return 2 * lax.rem(ring + dz, rings) + lax.rem(lane_y + dy, 2)

    def chip_from(step):
        dz, dy = hops[step]
        return 2 * lax.rem(ring - dz + rings, rings) + lax.rem(lane_y + dy, 2)

    def block_of(region):
        return everyone.at[pl.ds(pl.multiple_of(region * offer, offer), offer)]

    def push(source, region, target, sem):
        return pltpu.make_async_remote_copy(
            src_ref=source,
            dst_ref=block_of(region),
            send_sem=sem,
            recv_sem=recv_sem.at[region],
            device_id={"region": target},
            device_id_type=pl.DeviceIdType.MESH,
        )

    def came(region):
        block = block_of(region)
        pltpu.make_async_copy(block, block, recv_sem.at[region]).wait()

    def to_chip(step):
        return push(pub, me, 2 * chip_to(step) + core, send_sem.at[step])

    def to_partner(step):
        region = 2 * chip_from(step) + core
        return push(block_of(region), region, 2 * chip + 1 - core, pass_sem.at[step])

    own_to_partner = push(pub, me, 2 * chip + 1 - core, pass_sem.at[len(hops)])
    for step in range(len(hops)):
        to_chip(step).start()
    own_to_partner.start()
    everyone[pl.ds(pl.multiple_of(me * offer, offer), offer), :] = pub[...]

    def scatter_rows(target, first, rows, values):
        for c in range(chunks):
            target[pl.ds(first * chunks + c, rows, stride=chunks), :] = values[:, c * LANES : (c + 1) * LANES]

    def gathered_rows(source, first, rows):
        return jnp.concatenate(
            [source[pl.ds(first * chunks + c, rows, stride=chunks), :] for c in range(chunks)], axis=1
        )

    def pick(target, table, index, first, count, table_too=None, index_too=None):
        def one(at, carry):
            row = table[pl.ds(index[0, first + at], chunks), :]
            if table_too is not None:
                row = row + table_too[pl.ds(index_too[0, first + at], chunks), :]
            target[pl.ds(at * chunks, chunks), :] = row
            return carry

        lax.fori_loop(0, count, one, 0, unroll=True)

    scaled = []
    for at, (name, source, target) in enumerate((
        ("recv_row", recv_row, receivers), ("send_row", send_row, senders),
        ("grecv_row", grecv_row, greceivers), ("gsend_row", gsend_row, gsenders),
    )):
        loads[name].wait()
        width = source.shape[1]
        scaled_rows[at, :, pl.ds(0, width)] = jnp.minimum(source[...], n) * chunks
        copy = pltpu.make_async_copy(scaled_rows.at[at, :, pl.ds(0, width)], target, index_sem.at[at])
        copy.start()
        scaled.append(copy)
    for at in range(8):
        loads[("vec", at)].wait()
    loads["w_r"].wait()
    scatter_rows(tab_r, 0, n, dot(own[...], w_pe[pl.ds(m, m), :]) + vec[0])
    loads["w_s"].wait()
    scatter_rows(tab_s, 0, n, dot(own[...], w_pe[pl.ds(0, m), :]))
    tab_s[pl.ds(n * chunks, SUB), :] = jnp.zeros((SUB, LANES), F32)
    gtab_s[pl.ds(n * chunks, SUB), :] = jnp.zeros((SUB, LANES), F32)
    for name in ("need", "gneed", "live"):
        loads[name].wait()
    for copy in scaled:
        copy.wait()
    need_col = column_of([need[k, s] + s * offer for s in range(regions) for k in range(pair)])
    gneed_col = column_of([gneed[j, k] + j * offer for j in range(len(OFFSETS)) for k in range(pair)])
    gneed_hot = lane_hot(gneed_col, 0, arrived.shape[0])
    loads["w_e"].wait()
    for start in range(0, edge_count, BLOCK):
        loads[("edges", start)].wait()
    for start in range(0, edge_count, BLOCK):
        rows = pl.ds(start, BLOCK)
        slot = picked.at[start // BLOCK % 2]
        pick(slot, tab_r, receivers, start, BLOCK, tab_s, senders)
        pre[rows, :] = 0.5 * (dot(edges[rows, :], w_pe[pl.ds(2 * m, m), :]) + gathered_rows(slot, 0, BLOCK))
        remote = row_mask(send_row[:, start : start + BLOCK] - n, up(slots))
        hot[rows, :] = jnp.transpose(remote)[:, :slots].astype(BF16)

    loads["gnodes"].wait()
    loads["w_de"].wait()
    scatter_rows(gtab_r, 0, g, dot(gnodes[...], w_de[pl.ds(m, m), :]) + vec[4])
    for start in range(0, gedge_count, GRID_BLOCK):
        remote = row_hot(gsend_row[:, start : start + GRID_BLOCK] - n, gslots)
        ghot[pl.ds(start, GRID_BLOCK), :] = lax.dot_general(
            remote, gneed_hot, (((0,), (0,)), ((), ())), preferred_element_type=F32
        ).astype(BF16)

    for step in range(len(hops)):
        came(2 * chip_from(step) + core)
        to_partner(step).start()
    for name in ("w_pn", "w_dn"):
        loads[name].wait()
    for name, w_out in (("w_po", w_po), ("w_pno", w_pno)):
        loads[name].wait()
        centre(w_out)
    w_pn[pl.ds(m, m), :] = w_pn[pl.ds(m, m), :] * 0.5
    w_dn[pl.ds(m, m), :] = w_dn[pl.ds(m, m), :] * 0.5
    npre[...] = 0.5 * (dot(own[...], w_pn[pl.ds(0, m), :]) + vec[2])
    npre_offer[...] = 0.5 * (dot(pub[...], w_pn[pl.ds(0, m), :]) + vec[2])
    gnpre[...] = 0.5 * (dot(gnodes[...], w_dn[pl.ds(0, m), :]) + vec[6])
    came(2 * chip + 1 - core)
    for step in range(len(hops)):
        came(2 * chip_from(step) + 1 - core)
    wanted = dot(lane_hot(need_col, 0, regions * offer), everyone[...])
    rem[...] = (0.5 * dot(wanted.astype(BF16), w_pe[pl.ds(0, m), :])).astype(BF16)

    for start in range(0, edge_count, BLOCK):
        rows = pl.ds(start, BLOCK)
        act = pre[rows, :] + dot(hot[rows, :], rem[...])
        message = normed(silu_of_half(act), w_po[...], vec[1]).astype(BF16) + edges[rows, :]
        place = lax.broadcasted_iota(I32, (1, BLOCK), 1) + start
        targets = jnp.where(place < live[0, 0], recv_row[:, start : start + BLOCK], -1)
        part = dot(row_hot(targets, n), message)
        total[...] = part if start == 0 else total[...] + part

    summed = total[...].astype(BF16)
    act = npre_offer[...] + dot(dot(offer_hot, summed).astype(BF16), w_pn[pl.ds(m, m), :])
    pub_out[...] = (pub[...].astype(F32) + normed(silu_of_half(act), w_pno[...], vec[3])).astype(BF16)
    copies = []
    for slot, offset in enumerate(OFFSETS):
        copy = pltpu.make_async_remote_copy(
            src_ref=pub_out,
            dst_ref=arrived.at[pl.ds(slot * offer, offer)],
            send_sem=out_send_sem.at[slot],
            recv_sem=out_recv_sem.at[slot],
            device_id={"region": lax.rem(me - offset + regions, regions)},
            device_id_type=pl.DeviceIdType.MESH,
        )
        copy.start()
        copies.append(copy)
    for name in ("gedges", "w_do", "w_dno"):
        loads[name].wait()
    act = npre[...] + dot(summed, w_pn[pl.ds(m, m), :])
    updated[...] = (own[...].astype(F32) + normed(silu_of_half(act), w_pno[...], vec[3])).astype(BF16)
    scatter_rows(gtab_s, 0, n, dot(updated[...], w_de[pl.ds(0, m), :]))
    for start in range(0, gedge_count, GRID_BLOCK):
        rows = pl.ds(start, GRID_BLOCK)
        slot = gpicked.at[start // GRID_BLOCK % 2]
        pick(slot, gtab_r, greceivers, start, GRID_BLOCK, gtab_s, gsenders)
        gpre[rows, :] = 0.5 * (dot(gedges[rows, :], w_de[pl.ds(2 * m, m), :]) + gathered_rows(slot, 0, GRID_BLOCK))
    centre(w_do)
    centre(w_dno)
    own_to_partner.wait_send()
    for step in range(len(hops)):
        to_chip(step).wait_send()
        to_partner(step).wait_send()
    for copy in copies:
        copy.wait()
    grem = (0.5 * dot(arrived[...], w_de[pl.ds(0, m), :])).astype(BF16)

    for start in range(0, gedge_count, GRID_BLOCK):
        rows = pl.ds(start, GRID_BLOCK)
        act = gpre[rows, :] + dot(ghot[rows, :], grem)
        message = normed(silu_of_half(act), w_do[...], vec[5]).astype(BF16) + gedges[rows, :]
        part = dot(row_hot(grecv_row[:, start : start + GRID_BLOCK], g), message)
        gtotal[...] = part if start == 0 else gtotal[...] + part


def finale(updated, gtotal, gnpre, gnodes, w_dn, w_dno, vec, mesh_out, grid_out, stage, sem):
    first = pltpu.make_async_copy(updated, mesh_out, sem.at[0])
    first.start()
    m = stage.shape[1]
    act = gnpre[...] + dot(gtotal[...].astype(BF16), w_dn[pl.ds(m, m), :])
    stage[...] = (
        gnodes[...].astype(F32) + normed(silu_of_half(act), w_dno[...], vec[7])
    ).astype(BF16)
    second = pltpu.make_async_copy(stage, grid_out, sem.at[1])
    second.start()
    first.wait()
    second.wait()


def local(
    mesh_nodes, mesh_edges, grid_nodes, grid_edges,
    boundary, mesh_need, mesh_sender, mesh_receiver, mesh_live,
    grid_need, grid_sender, grid_receiver,
    *weights,
):
    regions = mesh_need.shape[1]
    pair = mesh_need.shape[2]
    offer = boundary.shape[1]
    n, m = mesh_nodes.shape
    g = grid_nodes.shape[0]
    edge_count = mesh_edges.shape[0]
    gedge_count = grid_edges.shape[0]
    slots = regions * pair
    gslots = len(OFFSETS) * pair
    chunks = m // LANES
    weights = [w if w.ndim == 2 else w.reshape(1, -1) for w in weights]

    sizes = (regions, offer, pair, n, m, edge_count, g, gedge_count)
    v = pltpu.VMEM
    s = pltpu.SMEM
    dma = pltpu.SemaphoreType.DMA
    scratch = [
        s((1, 1), I32), s((1, offer), I32), s((pair, regions), I32), s((len(OFFSETS), pair), I32),
        s((1, edge_count), I32), s((1, edge_count), I32), s((1, gedge_count), I32), s((1, gedge_count), I32),
        v((n, m), BF16), v((edge_count, m), BF16), v((gedge_count, m), BF16),
        v((1, edge_count), I32), v((1, edge_count), I32), v((1, gedge_count), I32), v((1, gedge_count), I32),
        v((4, 1, edge_count), I32),
        v((3 * m, m), BF16), v((m, m), BF16), v((2 * m, m), BF16), v((m, m), BF16),
        v((3 * m, m), BF16), v((m, m), BF16),
        v((n * chunks + SUB, LANES), F32), v((n * chunks, LANES), F32),
        v((n * chunks + SUB, LANES), F32), v((g * chunks, LANES), F32),
        v((2, BLOCK * chunks, LANES), F32), v((2, GRID_BLOCK * chunks, LANES), F32),
        v((edge_count, m), F32), v((gedge_count, m), F32), v((n, m), F32), v((offer, m), F32),
        v((n, m), F32),
        v((edge_count, slots), BF16), v((gedge_count, len(OFFSETS) * offer), BF16), v((slots, m), BF16),
        v((offer, m), BF16), v((regions * offer, m), BF16), v((offer, m), BF16),
        v((len(OFFSETS) * offer, m), BF16),
        dma((44,)), dma((4,)), dma((regions // 2,)), dma((regions // 2,)), dma((regions,)),
        dma((len(OFFSETS),)), dma((len(OFFSETS),)),
    ]
    hbm = pl.BlockSpec(memory_space=pltpu.HBM)
    handed = pl.pallas_call(
        functools.partial(kernel, sizes),
        out_shape=(
            v((n, m), BF16), v((g, m), F32), v((g, m), F32), v((g, m), BF16),
            v((2 * m, m), BF16), v((m, m), BF16), v((8, 1, m), F32),
        ),
        in_specs=[hbm] * 28,
        out_specs=(pl.BlockSpec(memory_space=pltpu.VMEM),) * 7,
        scratch_shapes=scratch,
        compiler_params=pltpu.CompilerParams(
            collective_id=0, has_side_effects=True, vmem_limit_bytes=56 * 1024 * 1024
        ),
        name="layer",
    )(
        mesh_live.reshape(1, 1), boundary, jnp.swapaxes(mesh_need[0], 0, 1), grid_need[0],
        mesh_nodes, mesh_edges, grid_nodes, grid_edges,
        mesh_sender, mesh_receiver, grid_sender, grid_receiver,
        *weights,
    )
    return pl.pallas_call(
        finale,
        out_shape=(jax.ShapeDtypeStruct((n, m), BF16), jax.ShapeDtypeStruct((g, m), BF16)),
        in_specs=[pl.BlockSpec(memory_space=pltpu.VMEM)] * 7,
        out_specs=(pl.BlockSpec(memory_space=pl.ANY),) * 2,
        scratch_shapes=[v((g, m), BF16), dma((2,))],
        compiler_params=pltpu.CompilerParams(vmem_limit_bytes=16 * 1024 * 1024),
        name="finale",
    )(*(pltpu.with_memory_space_constraint(one, pltpu.VMEM) for one in handed))


def solution(mesh):
    both = P(("member", "region"), None)
    by = P("region", None)
    return jax.shard_map(
        local,
        mesh=mesh,
        in_specs=(
            both, by, both, by, by, P("region", None, None), by, by, P("region"),
            P("region", None, None), by, by,
        ) + (P(),) * 16,
        out_specs=(both, both),
        check_vma=False,
    )
```

time: 35.8 us -> 29.3 us (0.82)
  local copies, waits for them, and re-layouts: 3.63 us -> 0 us
  Pallas kernels: 30.7 us -> 27.8 us
    unnamed x2 -> x0, local copies, waits for them, and re-layouts: 3.63 us -> none
    pallas_call x1 -> x2, Pallas kernels: 30.7 us -> 27.8 us  [the longest x1 26.3 us: local(): pl.pallas_call(functools.partial(kernel, sizes), out_shape=(v((n, m), BF1...]
where the time goes in v2:
time: 29.3 us; the launch traced here: 29.1 us
  Pallas kernels  27.8 us (95%)
  between operations  1.29 us (4%)
    pallas_call x1, Pallas kernels, local(): pl.pallas_call(functools.partial(kernel, sizes), out_shape=(v((n, m), BF1...  26.3 us
    pallas_call x1, Pallas kernels, local(): pl.pallas_call(finale, out_shape=(jax.ShapeDtypeStruct((n, m), BF16), jax...  1.54 us

profile of v2, /device:TPU:0, one launch (start us, length us, event | category | flops | bytes accessed | tf_op | source)
XLA Modules:
  0.0 29.1 jit_solution(6214115989291104953)
XLA Ops:
  1.3 26.3 %layer.1 = (bf16[512,512]{1,0:T(8,128)(2,1)S(1)}, f32[384,512]{1,0:T(8,128)S(1)}, f32[384,512]{1,0:T(8,128)S(1)}, bf16[384,512]{1,0:T(8,128)(2,1)S(1)}, bf16[102...) custom-call(s32[1,1]{1,0:T(1,128)} %bitcast.13.live_hbm, s32[1,32]{1,0:T(1,128)} %boundary_hbm.1, ...), custom_call_target="tpu_custom_call" | custom-call | tf_op jit(solution)/shard_map/layer/pallas_call | solution.py:397
  27.6 1.5 %finale.1 = (bf16[512,512]{1,0:T(8,128)(2,1)}, bf16[384,512]{1,0:T(8,128)(2,1)}) custom-call(bf16[512,512]{1,0:T(8,128)(2,1)S(1)} %get-tuple-element.9.updated, f32[384,512]{1,0:T(8,128)S(1)} %get-tuple-element.10.gtotal, f32[384,512]{1,0:T(8,128)S(1)} %get-tuple-element.11.gnpre, bf16[384,512]{1,0:T(8,128)(2,1)S(1)} %get-tuple-element.12.gnodes, ...), custom_call_target="tpu_custom_call" | custom-call | tf_op jit(solution)/shard_map/finale/pallas_call | solution.py:416

commit v3 on v2

--- a/solution.py
+++ b/solution.py
@@ -13,7 +13,7 @@
 OFFSETS = (-2, -1, 1, 2)
 LANES = 128
 SUB = 8
-BLOCK = 512
+BLOCK = 1024
 GRID_BLOCK = 384
 
 
@@ -330,12 +330,9 @@
         copy.wait()
     grem = (0.5 * dot(arrived[...], w_de[pl.ds(0, m), :])).astype(BF16)
 
-    for start in range(0, gedge_count, GRID_BLOCK):
-        rows = pl.ds(start, GRID_BLOCK)
-        act = gpre[rows, :] + dot(ghot[rows, :], grem)
-        message = normed(silu_of_half(act), w_do[...], vec[5]).astype(BF16) + gedges[rows, :]
-        part = dot(row_hot(grecv_row[:, start : start + GRID_BLOCK], g), message)
-        gtotal[...] = part if start == 0 else gtotal[...] + part
+    act = gpre[...] + dot(ghot[...], grem)
+    message = normed(silu_of_half(act), w_do[...], vec[5]).astype(BF16) + gedges[...]
+    gtotal[...] = dot(row_hot(grecv_row[...], g), message)
 
 
 def finale(updated, gtotal, gnpre, gnodes, w_dn, w_dno, vec, mesh_out, grid_out, stage, sem):

time: 29.3 us -> 28.1 us (0.959)
  Pallas kernels: 27.8 us -> 26.6 us
    pallas_call x1, Pallas kernels: 26.3 us -> 25.1 us  [local(): pl.pallas_call(functools.partial(kernel, sizes), out_shape=(v((n, m), BF1...]
where the time goes in v3:
time: 28.1 us; the launch traced here: 27.9 us
  Pallas kernels  26.6 us (95%)
  between operations  1.29 us (5%)
    pallas_call x1, Pallas kernels, local(): pl.pallas_call(functools.partial(kernel, sizes), out_shape=(v((n, m), BF1...  25.1 us
    pallas_call x1, Pallas kernels, local(): pl.pallas_call(finale, out_shape=(jax.ShapeDtypeStruct((n, m), BF16), jax...  1.54 us

profile of v3, /device:TPU:0, one launch (start us, length us, event | category | flops | bytes accessed | tf_op | source)
XLA Modules:
  0.0 27.9 jit_solution(8473638790299019026)
XLA Ops:
  1.3 25.1 %layer.1 = (bf16[512,512]{1,0:T(8,128)(2,1)S(1)}, f32[384,512]{1,0:T(8,128)S(1)}, f32[384,512]{1,0:T(8,128)S(1)}, bf16[384,512]{1,0:T(8,128)(2,1)S(1)}, bf16[102...) custom-call(s32[1,1]{1,0:T(1,128)} %bitcast.13.live_hbm, s32[1,32]{1,0:T(1,128)} %boundary_hbm.1, ...), custom_call_target="tpu_custom_call" | custom-call | tf_op jit(solution)/shard_map/layer/pallas_call | solution.py:394
  26.4 1.5 %finale.1 = (bf16[512,512]{1,0:T(8,128)(2,1)}, bf16[384,512]{1,0:T(8,128)(2,1)}) custom-call(bf16[512,512]{1,0:T(8,128)(2,1)S(1)} %get-tuple-element.9.updated, f32[384,512]{1,0:T(8,128)S(1)} %get-tuple-element.10.gtotal, f32[384,512]{1,0:T(8,128)S(1)} %get-tuple-element.11.gnpre, bf16[384,512]{1,0:T(8,128)(2,1)S(1)} %get-tuple-element.12.gnodes, ...), custom_call_target="tpu_custom_call" | custom-call | tf_op jit(solution)/shard_map/finale/pallas_call | solution.py:413
